TPU v7x, 256 devices: a whole 4x4x8 slice. The times are simulated.
256 devices in a mesh: row: 8 (over y, x_lo), col: 32 (over x_hi, z, core).
Axes of the slice: x: 4 (x_hi: 2, x_lo: 2; x = x_hi * 2 + x_lo), y: 4, z: 8, core: 2. Of those that a mesh axis runs over, the one named last changes fastest.
Arguments:
- inverse_state: float32 [4, 2048, 1, 8192], P(None, 'row', None, 'col')
- row_seeds: int32 [2, 4, 2048], P(None, None, 'row'), may hold values from 0 to 31
- col_seeds: int32 [2, 1, 8192], P(None, None, 'col'), may hold values from 0 to 31
Outputs:
- inverse: float32 [4, 2048, 1, 8192], P(None, 'row', None, 'col')
All inputs are finite; a program needn't handle non-finite values.
Results may differ from a plain program's by a relative error of at most 0.0002.
Values sent between devices are 32-bit elements; how exact they have to be, the bound alone decides.
No kernel may reach another device: no remote copies, remote signals or barrier semaphores. Data moves between devices by JAX's collectives and lax.ppermute only.
A program may use at most 64 MiB of HBM per device.

v0:
```python
import jax
import jax.numpy as jnp
from jax import lax
from jax.experimental import pallas as pl
from jax.experimental.pallas import tpu as pltpu
from jax.sharding import PartitionSpec as P


LIMIT = 64
WARM = 8
root_half = 0.7071067811865476
HIGHEST = lax.Precision.HIGHEST


def seed_values(seeds):
    return (2.0 * seeds.astype(jnp.float32) - 31.0) / 16.0


def halves_level(parts, scales, groups):
    count = parts.shape[0]
    half = count // (2 * groups)
    shaped = parts.reshape((groups, 2, half) + parts.shape[1:])
    factor = scales.reshape((groups, 2, half) + scales.shape[1:])
    upper = factor[:, 0] * shaped[:, 0]
    lower = factor[:, 1] * shaped[:, 1]
    return (jnp.stack([upper + lower, upper - lower], axis=1) * root_half).reshape(parts.shape)


def butterfly(parts, scales):
    return halves_level(halves_level(parts, scales[0], 1), scales[1], 2)


def kdot(a, b, dims=(((1,), (0,)), ((), ())), precision=HIGHEST):
    return lax.dot_general(a, b, dims, precision=precision, preferred_element_type=jnp.float32)


def invert_into(p_ref, x_ref, e_ref):
    size = p_ref.shape[0]
    scale = 1.0 / jnp.max(jnp.abs(p_ref[...]))
    p_ref[...] = p_ref[...] * scale
    gram = kdot(p_ref[...], p_ref[...], (((1,), (1,)), ((), ())))
    factor = 1.9 / jnp.max(jnp.sum(jnp.abs(gram), axis=0, keepdims=True))

    def start():
        x_ref[...] = p_ref[...].T * factor

    def residual(precision):
        row = lax.broadcasted_iota(jnp.int32, (size, size), 0)
        column = lax.broadcasted_iota(jnp.int32, (size, size), 1)
        product = kdot(p_ref[...], x_ref[...], precision=precision)
        e_ref[...] = jnp.where(row == column, 1.0, 0.0) - product

    def advance(precision):
        x_ref[...] += kdot(x_ref[...], e_ref[...], precision=precision)

    def exact_error():
        residual(HIGHEST)
        e = e_ref[...]
        return jnp.sum(e * e)

    start()

    @pl.loop(0, WARM)
    def _(_):
        residual(lax.Precision.DEFAULT)
        advance(lax.Precision.DEFAULT)

    error = exact_error()
    failed = jnp.logical_not(error < 0.5)

    @pl.when(failed)
    def _():
        start()
        residual(HIGHEST)

    def unfinished(carry):
        count, error = carry
        return (count < LIMIT) & jnp.logical_not(error < 1e-7)

    def again(carry):
        advance(HIGHEST)
        return carry[0] + 1, exact_error()

    lax.while_loop(unfinished, again, (0, jnp.where(failed, 1.0, error)))
    advance(HIGHEST)
    x_ref[...] = x_ref[...] * scale


def first_kernel(odd_ref, near_ref, far_ref, first_ref, left_ref, right_ref, schur_ref, p_ref, e_ref):
    odd = odd_ref[0] == 1

    def part(i, j):
        near, far = near_ref[:, i], far_ref[:, i]
        return jnp.where(odd == (j == 1), near, far).reshape(p_ref.shape)

    p_ref[...] = part(0, 0)
    invert_into(p_ref, first_ref, e_ref)
    left_ref[...] = kdot(part(1, 0), first_ref[...])
    p_ref[...] = part(0, 1)
    right_ref[...] = kdot(first_ref[...], p_ref[...])
    schur_ref[...] = part(1, 1) - kdot(left_ref[...], p_ref[...])


def second_kernel(schur_ref, first_ref, left_ref, right_ref, rows_ref, out_ref, p_ref, x_ref, e_ref):
    p_ref[...] = schur_ref[...]
    invert_into(p_ref, x_ref, e_ref)
    e_ref[...] = rows_ref[1] - kdot(left_ref[...], rows_ref[0])
    out_ref[1] = kdot(x_ref[...], e_ref[...])
    out_ref[0] = kdot(first_ref[...], rows_ref[0]) - kdot(right_ref[...], out_ref[1])


def last_kernel(place_ref, base_ref, own_ref, across_ref, twin_ref, other_ref, rows_ref, out_ref):
    odd, half = place_ref[0] == 1, place_ref[1]
    count, blocks, strip, size = own_ref.shape
    tall = count * strip
    for a in range(blocks):
        for side, (same, swapped) in enumerate([(own_ref, twin_ref), (across_ref, other_ref)]):
            one, two = same[:, a].reshape(tall, size), swapped[:, a].reshape(tall, size)
            update = kdot(jnp.where(odd, two, one), rows_ref[0])
            update += kdot(jnp.where(odd, one, two), rows_ref[1])
            top = (half if side == 0 else 1 - half) * tall
            value = base_ref[a, pl.ds(pl.multiple_of(top, tall), tall), :] - update
            for lane in range(size // 128):
                at = pl.ds((a * size + top) * (size // 128) + lane, tall, stride=size // 128)
                out_ref[at, :] = value[:, lane * 128 : (lane + 1) * 128]


def call(kernel, out_shape, scratch, flops, *args):
    smem = [pl.BlockSpec(memory_space=pltpu.SMEM)] if args[0].dtype == jnp.int32 else []
    rest = len(args) - len(smem)
    return pl.pallas_call(
        kernel,
        out_shape=out_shape,
        in_specs=smem + [pl.BlockSpec(memory_space=pltpu.VMEM)] * rest,
        out_specs=jax.tree.map(lambda _: pl.BlockSpec(memory_space=pltpu.VMEM), out_shape),
        scratch_shapes=scratch,
        cost_estimate=pl.CostEstimate(flops=flops, bytes_accessed=1 << 20, transcendentals=0),
    )(*args)


def after(value, *earlier):
    return lax.optimization_barrier((value, *earlier))[0]


def per_device(inverse_state, row_seeds, col_seeds):
    blocks, block = inverse_state.shape[:2]
    rows, cols = lax.axis_size("row"), lax.axis_size("col")
    row, col = lax.axis_index("row"), lax.axis_index("col")
    half, ring, last = cols // 2, cols // 4, blocks - 1
    side, place, core = col // half, col % half // 2, col % 2
    rings = [
        [s * half + p * 2 + c for p in range(ring)] for s in range(2) for c in range(2)
    ]
    state = inverse_state.reshape(blocks, block, block)
    identity = jnp.eye(block, dtype=jnp.float32)
    pivot_col = col >= cols - 2
    diagonal = (col - cols == row - rows) & pivot_col
    row_scales = seed_values(row_seeds)[..., None]
    col_scales = seed_values(col_seeds).reshape(2, 1, block)
    smem = jnp.stack([core, side]).astype(jnp.int32)

    def send(value, pairs, axis="col"):
        return lax.ppermute(value, axis, pairs)

    def flip(value, bit):
        return send(value, [(i, i ^ bit) for i in range(cols)])

    def exchange(parts, axis, groups=None):
        return lax.all_to_all(parts, axis, 0, 0, axis_index_groups=groups)

    def spread(part, count, axis, groups=None):
        return exchange(jnp.broadcast_to(part, (count,) + part.shape), axis, groups)

    def joined(top, own, partner):
        return jnp.where(top, own + partner, partner - own)

    span_one, span_two = half, half // 2
    top_one, top_two = col // span_one % 2 == 0, col // span_two % 2 == 0

    tail = state[last]
    strips = exchange(tail.reshape(rows, block // rows, block), "row")[rows - 2 :]
    crossed = send(strips, [(i, i - half) for i in (cols - 2, cols - 1)])
    both = jnp.where(place == ring - 1, jnp.where(side == 1, strips, crossed), 0.0)

    left = jnp.where(
        diagonal,
        jnp.concatenate([state[:last], (tail - identity)[None]], 0),
        state,
    )
    left = butterfly(left, row_scales)
    tall = block // 2
    crossed = send(left[:, :tall], [(i, i - half) for i in (cols - 2, cols - 1)])
    own_half = jnp.where(side == 1, left[:, tall:], after(crossed, both))

    def hops(step):
        sources = range(2 * step - 1, ring, 2 * step)
        return [(group[p], group[p - step]) for group in rings for p in sources]

    steps = [ring >> (i + 1) for i in range(ring.bit_length() - 1)]

    ready = [both]
    for step in steps:
        ready.append(ready[-1] + send(ready[-1], hops(step)))
    strips = ready[-1]

    piece = own_half
    for i, step in enumerate(steps):
        wide = piece.shape[1] // 2
        moved = after(send(piece[:, :wide], hops(step)), ready[i + 1])
        piece = jnp.where(place % (2 * step) == 2 * step - 1, piece[:, wide:], moved)

    cleared = jnp.where(pivot_col, jnp.where(diagonal, identity, 0.0), tail) * col_scales[0]
    tail_one = joined(top_one, cleared, flip(cleared, span_one)) * root_half
    tail_one = tail_one * col_scales[1]
    partner = after(flip(tail_one, span_two), strips)
    tail_moved = joined(top_two, tail_one, partner) * root_half

    def row_fan(step):
        pairs = [(i, (i + 2 * step) % rows) for i in (rows - 2, rows - 1)]
        return send(tail_moved, pairs, "row")

    near = row_fan(1) + row_fan(2) + row_fan(3)
    near = jnp.where(row >= rows - 2, tail_moved, near)
    far = send(near, [(i, i ^ 1) for i in range(rows)], "row")
    odd_row = row % 2 == 1
    pivot_rows = jnp.stack([jnp.where(odd_row, far, near), jnp.where(odd_row, near, far)])

    pivot_near = spread(strips, rows, "row")
    pivot_near = after(pivot_near, piece, near)
    pivot_far = flip(pivot_near, 1)
    left_own = spread(after(piece, pivot_near), ring, "col", rings)

    second = col_scales[1]
    second_one = flip(second, span_one)
    near_pair = jnp.stack([second, second_one])
    far_pair = flip(near_pair, span_two)
    head = jnp.where(pivot_col, 0.0, state[:last]) * col_scales[0]
    head_far = after(flip(head, span_two), pivot_near)
    head_own = joined(top_two, near_pair[0] * head, far_pair[0] * head_far)
    head_sent = joined(top_two, near_pair[1] * head, far_pair[1] * head_far)
    head_partner = flip(head_sent, span_one)

    matrix = jax.ShapeDtypeStruct((block, block), jnp.float32)
    buffer = pltpu.VMEM((block, block), jnp.float32)
    work = 2 * block**3
    first, below, over, schur = call(
        first_kernel, [matrix] * 4, [buffer] * 2, 160 * work, smem, pivot_near, pivot_far
    )
    left_own = after(left_own, first)
    left_across = flip(left_own, span_one)
    left_twin = flip(left_own, 1)
    right = call(
        second_kernel,
        jax.ShapeDtypeStruct((2, block, block), jnp.float32),
        [buffer] * 3,
        160 * work,
        schur,
        first,
        below,
        over,
        pivot_rows,
    )
    left_across, head_partner = after(left_across, right), after(head_partner, right)
    left_other = flip(left_across, 1)
    head_moved = joined(top_one, head_own, head_partner) * (root_half * root_half)
    moved = butterfly(jnp.concatenate([head_moved, tail_moved[None]], 0), row_scales)
    result = call(
        last_kernel,
        jax.ShapeDtypeStruct((blocks * block * block // 128, 128), jnp.float32),
        [],
        6 * 8 * work,
        smem,
        moved,
        left_own,
        left_across,
        left_twin,
        left_other,
        right,
    )
    return result.reshape(inverse_state.shape)


def solution(mesh):
    placed = (P(None, "row", None, "col"), P(None, None, "row"), P(None, None, "col"))

    return jax.shard_map(
        per_device,
        mesh=mesh,
        in_specs=placed,
        out_specs=P(None, "row", None, "col"),
        check_vma=False,
    )
```

profile of v0, /device:TPU:1, one launch (start us, length us, event | category | flops | bytes accessed | tf_op | source)
XLA Modules:
  0.0 152.3 jit_solution(7341550624402665792)
XLA Ops:
  3.3 3.6 %collective-permute-start.11 = (f32[256,256]{1,0:T(8,128)}, f32[256,256]{1,0:T(8,128)}, u32[]{:S(2)}, u32[]{:S(2)}) collective-permute-start(f32[256,256]{1,0:T(8,128)} %fusion.5), channel_id=1, source_target_pairs={{0,16},{1,17},{2,18},{3,19},{4,20},{5,21},{6,22},{7,23},{8,24},{9,... | collective-permute-start | bytes 786440 | tf_op jit(solution)/shard_map/ppermute | solution.py:163
  7.6 4.2 %all-to-all-start = ((f32[8,32,256]{2,1,0:T(8,128)}), f32[8,32,256]{2,1,0:T(8,128)S(1)}, u32[]{:S(2)}, u32[]{:S(2)}) async-start(f32[8,32,256]{2,1,0:T(8,128)} %bitcast.8), calls=%async_computation | async-start | bytes 524288 | tf_op jit(solution)/shard_map/all_to_all | solution.py:169
  13.3 6.9 %collective-permute-start.2 = (f32[3,256,256]{2,1,0:T(8,128)}, f32[3,256,256]{2,1,0:T(8,128)}, u32[]{:S(2)}, u32[]{:S(2)}) collective-permute-start(f32[3,256,256]{2,1,0:T(8,128)} %select_multiply_fusion.1), channel_id=1, source_target_pairs={{0,8},{1,9},{2,10},{3,11},{4,12},{5,13},{6,14},{7,15},{8,0},{9,1},... | collective-permute-start | bytes 2359304 | tf_op jit(solution)/shard_map/ppermute | solution.py:163
  23.0 1.8 %collective-permute-start = (f32[1,256]{1,0:T(1,128)}, f32[1,256]{1,0:T(1,128)}, u32[]{:S(2)}, u32[]{:S(2)}) collective-permute-start(f32[1,256]{1,0:T(1,128)} %get-tuple-element.53), channel_id=1, source_target_pairs={{0,16},{1,17},{2,18},{3,19},{4,20},{5,21},{6,22},{7,23},{8,24},{9,... | collective-permute-start | bytes 3080 | tf_op jit(solution)/shard_map/ppermute | solution.py:163
  29.9 1.3 collective-permute-start.6
  32.7 5.3 %collective-permute-start.1 = (f32[2,1,256]{2,1,0:T(1,128)S(1)}, f32[2,1,256]{2,1,0:T(1,128)S(1)}, u32[]{:S(2)}, u32[]{:S(2)}) collective-permute-start(f32[2,1,256]{2,1,0:T(1,128)S(1)} %pad_maximum_fusion.3), channel_id=1, source_target_pairs={{0,8},{1,9},{2,10},{3,11},{4,12},{5,13},{6,14},{7,15},{8,0},{9,1},... | collective-permute-start | bytes 6152 | tf_op jit(solution)/shard_map/ppermute | solution.py:163
  38.0 33.2 %collective-permute-done.6 = f32[2,32,256]{2,1,0:T(8,128)S(1)} collective-permute-done((f32[2,32,256]{2,1,0:T(8,128)S(1)}, f32[2,32,256]{2,1,0:T(8,128)S(1)}, u32[]{:S(2)}, u32[]{:S(2)}) %collective-permute-start.6) | collective-permute-done | bytes 65568 | tf_op jit(solution)/shard_map/ppermute | solution.py:163
  72.0 1.3 collective-permute-start.13
  75.6 7.2 %all-to-all-start.1 = ((f32[8,2,32,256]{3,2,1,0:T(8,128)}), f32[8,2,32,256]{3,2,1,0:T(8,128)}, u32[]{:S(2)}, u32[]{:S(2)}) async-start(f32[8,2,32,256]{3,2,1,0:T(8,128)} %broadcast_in_dim.25), calls=%async_computation.1 | async-start | bytes 1048576 | tf_op jit(solution)/shard_map/all_to_all | solution.py:169
  82.8 1.3 collective-permute-start.10
  84.2 1.5 %collective-permute-start.18 = (f32[256,256]{1,0:T(8,128)S(1)}, f32[256,256]{1,0:T(8,128)}, u32[]{:S(2)}, u32[]{:S(2)}) collective-permute-start(f32[256,256]{1,0:T(8,128)S(1)} %add_select_fusion), channel_id=1, source_target_pairs={{0,32},{32,0},{64,96},{96,64},{128,160},{160,128},{192,224},{224,1... | collective-permute-start | bytes 786440 | tf_op jit(solution)/shard_map/ppermute | solution.py:163
  85.7 2.5 %collective-permute-done.10 = f32[4,16,256]{2,1,0:T(8,128)S(1)} collective-permute-done((f32[4,16,256]{2,1,0:T(8,128)S(1)}, f32[4,16,256]{2,1,0:T(8,128)S(1)}, u32[]{:S(2)}, u32[]{:S(2)}) %collective-permute-start.10) | collective-permute-done | bytes 65568 | tf_op jit(solution)/shard_map/ppermute | solution.py:163
  88.2 3.8 %all-to-all-done.1.near_ref = f32[8,2,32,256]{3,2,1,0:T(8,128)} async-done(((f32[8,2,32,256]{3,2,1,0:T(8,128)}), f32[8,2,32,256]{3,2,1,0:T(8,128)}, u32[]{:S(2)}, u32[]{:S(2)}) %all-to-all-start.1) | async-done | bytes 524320 | tf_op jit(solution)/shard_map/all_to_all | solution.py:169
  92.0 3.4 %collective-permute-start.17 = (f32[8,2,32,256]{3,2,1,0:T(8,128)}, f32[8,2,32,256]{3,2,1,0:T(8,128)}, u32[]{:S(2)}, u32[]{:S(2)}) collective-permute-start(f32[8,2,32,256]{3,2,1,0:T(8,128)} %all-to-all-done.1.near_ref), channel_id=1, source_target_pairs={{0,1},{1,0},{2,3},{3,2},{4,5},{5,4},{6,7},{7,6},{8,9},{9,8},{10,11... | collective-permute-start | bytes 1572872 | tf_op jit(solution)/shard_map/ppermute | solution.py:163
  95.4 1.3 subtract_select_fusion
  96.7 1.8 %collective-permute-start.16 = (f32[3,256,256]{2,1,0:T(8,128)S(1)}, f32[3,256,256]{2,1,0:T(8,128)S(1)}, u32[]{:S(2)}, u32[]{:S(2)}) collective-permute-start(f32[3,256,256]{2,1,0:T(8,128)S(1)} %subtract_select_fusion), channel_id=1, source_target_pairs={{0,16},{1,17},{2,18},{3,19},{4,20},{5,21},{6,22},{7,23},{8,24},{9,... | collective-permute-start | bytes 2359304 | tf_op jit(solution)/shard_map/ppermute | solution.py:163
  99.4 8.2 %all-to-all-start.2 = ((f32[8,4,16,256]{3,2,1,0:T(8,128)}), f32[8,4,16,256]{3,2,1,0:T(8,128)S(1)}, u32[]{:S(2)}, u32[]{:S(2)}) async-start(f32[8,4,16,256]{3,2,1,0:T(8,128)} %broadcast_in_dim.28), calls=%async_computation.2 | async-start | bytes 1048576 | tf_op jit(solution)/shard_map/all_to_all | solution.py:169
  109.4 9.4 %shard_map.37 = (f32[256,256]{1,0:T(8,128)}, f32[256,256]{1,0:T(8,128)}, f32[256,256]{1,0:T(8,128)}, f32[256,256]{1,0:T(8,128)}) custom-call(s32[2]{0:T(128)} %pad_add_fusion.odd_ref.place_ref, f32[8,2,32,256]{3,2,1,0:T(8,128)} %all-to-all-done.1.near_ref, f32[8,2,32,256]{3,2,1,0:T(8,128)} %collective-permute-done.17.far_ref), custom_call_target="tpu_custom_call" | custom-call | flops 5368709120 | bytes 1048576 | tf_op jit(solution)/shard_map/pallas_call | solution.py:131
  118.8 9.7 %shard_map.38.rows_ref = f32[2,256,256]{2,1,0:T(8,128)} custom-call(f32[256,256]{1,0:T(8,128)} %get-tuple-element.27.schur_ref, f32[256,256]{1,0:T(8,128)} %get-tuple-element.28.first_ref, f32[256,256]{1,0:T(8,128)} %get-tuple-element.29.left_ref, f32[256,256]{1,0:T(8,128)} %get-tuple-element.30.right_ref, f32[2,256,256]{2,1,0:T(8,128)} %pad_maximum_fusion.2.rows_ref), custom_call_target="tpu_custom_call" | custom-call | flops 5368709120 | bytes 1048576 | tf_op jit(solution)/shard_map/pallas_call | solution.py:131
  128.5 1.3 collective-permute-start.19
  129.8 1.4 select_multiply_fusion
  132.5 10.5 %collective-permute-done.19.across_ref = f32[8,4,16,256]{3,2,1,0:T(8,128)S(1)} collective-permute-done((f32[8,4,16,256]{3,2,1,0:T(8,128)S(1)}, f32[8,4,16,256]{3,2,1,0:T(8,128)S(1)}, u32[]{:S(2)}, u32[]{:S(2)}) %collective-permute-start.19) | collective-permute-done | bytes 524320 | tf_op jit(solution)/shard_map/ppermute | solution.py:163
  143.0 1.4 collective-permute-start.21
  147.4 4.9 %shard_map.39 = f32[2048,128]{1,0:T(8,128)} custom-call(s32[2]{0:T(128)} %pad_add_fusion.odd_ref.place_ref, f32[4,256,256]{2,1,0:T(8,128)} %bitcast.68, f32[8,4,16,256]{3,2,1,0:T(8,128)} %copy-done.1, f32[8,4,16,256]{3,2,1,0:T(8,128)} %copy-done.9, f32[8,4,16,256]{3,2,1,0:T(8,128)} %copy-done.10, f32[8,4,16,256]{3,2,1,0:T(8,128)} %copy-done.11, ...), custom_call_target="tpu_custom_call" | custom-call | flops 1610612736 | bytes 1048576 | tf_op jit(solution)/shard_map/pallas_call | solution.py:131
  (106 shorter events, 24.6 us)
Async XLA Ops:
  3.3 25.5 %collective-permute-start.11 = (f32[256,256]{1,0:T(8,128)}, f32[256,256]{1,0:T(8,128)}, u32[]{:S(2)}, u32[]{:S(2)}) collective-permute-start(f32[256,256]{1,0:T(8,128)} %fusion.5), channel_id=1, source_target_pairs={{0,16},{1,17},{2,18},{3,19},{4,20},{5,21},{6,22},{7,23},{8,24},{9,... | collective-permute-start | bytes 786440 | tf_op jit(solution)/shard_map/ppermute | solution.py:163
  7.6 17.3 %all-to-all-start = ((f32[8,32,256]{2,1,0:T(8,128)}), f32[8,32,256]{2,1,0:T(8,128)S(1)}, u32[]{:S(2)}, u32[]{:S(2)}) async-start(f32[8,32,256]{2,1,0:T(8,128)} %bitcast.8), calls=%async_computation | async-start | bytes 524288 | tf_op jit(solution)/shard_map/all_to_all | solution.py:169
  13.3 82.1 %collective-permute-start.2 = (f32[3,256,256]{2,1,0:T(8,128)}, f32[3,256,256]{2,1,0:T(8,128)}, u32[]{:S(2)}, u32[]{:S(2)}) collective-permute-start(f32[3,256,256]{2,1,0:T(8,128)} %select_multiply_fusion.1), channel_id=1, source_target_pairs={{0,8},{1,9},{2,10},{3,11},{4,12},{5,13},{6,14},{7,15},{8,0},{9,1},... | collective-permute-start | bytes 2359304 | tf_op jit(solution)/shard_map/ppermute | solution.py:163
  22.3 8.9 %collective-permute-start.7 = (f32[4,128,256]{2,1,0:T(8,128)S(1)}, f32[4,128,256]{2,1,0:T(8,128)S(1)}, u32[]{:S(2)}, u32[]{:S(2)}) collective-permute-start(f32[4,128,256]{2,1,0:T(8,128)S(1)} %slice.147), channel_id=1, source_target_pairs={{30,14},{31,15},{62,46},{63,47},{94,78},{95,79},{126,110},{127,111... | collective-permute-start | bytes 1572872 | tf_op jit(solution)/shard_map/ppermute | solution.py:163
  23.0 9.0 %collective-permute-start = (f32[1,256]{1,0:T(1,128)}, f32[1,256]{1,0:T(1,128)}, u32[]{:S(2)}, u32[]{:S(2)}) collective-permute-start(f32[1,256]{1,0:T(1,128)} %get-tuple-element.53), channel_id=1, source_target_pairs={{0,16},{1,17},{2,18},{3,19},{4,20},{5,21},{6,22},{7,23},{8,24},{9,... | collective-permute-start | bytes 3080 | tf_op jit(solution)/shard_map/ppermute | solution.py:163
  24.8 1.9 %collective-permute-start.3 = (f32[2,32,256]{2,1,0:T(8,128)S(1)}, f32[2,32,256]{2,1,0:T(8,128)S(1)}, u32[]{:S(2)}, u32[]{:S(2)}) collective-permute-start(f32[2,32,256]{2,1,0:T(8,128)S(1)} %slice.139), channel_id=1, source_target_pairs={{30,14},{31,15},{62,46},{63,47},{94,78},{95,79},{126,110},{127,111... | collective-permute-start | bytes 196616 | tf_op jit(solution)/shard_map/ppermute | solution.py:163
  28.1 1.8 %collective-permute-start.5 = (f32[2,32,256]{2,1,0:T(8,128)S(1)}, f32[2,32,256]{2,1,0:T(8,128)S(1)}, u32[]{:S(2)}, u32[]{:S(2)}) collective-permute-start(f32[2,32,256]{2,1,0:T(8,128)S(1)} %add.90), channel_id=1, source_target_pairs={{6,2},{14,10},{7,3},{15,11},{22,18},{30,26},{23,19},{31,27},{38,34... | collective-permute-start | bytes 196616 | tf_op jit(solution)/shard_map/ppermute | solution.py:163
  29.8 41.4 %collective-permute-start.12 = (f32[256,256]{1,0:T(8,128)S(1)}, f32[256,256]{1,0:T(8,128)S(1)}, u32[]{:S(2)}, u32[]{:S(2)}) collective-permute-start(f32[256,256]{1,0:T(8,128)S(1)} %select_multiply_fusion.3), channel_id=1, source_target_pairs={{0,8},{1,9},{2,10},{3,11},{4,12},{5,13},{6,14},{7,15},{8,0},{9,1},... | collective-permute-start | bytes 786440 | tf_op jit(solution)/shard_map/ppermute | solution.py:163
  29.9 41.3 %collective-permute-start.6 = (f32[2,32,256]{2,1,0:T(8,128)S(1)}, f32[2,32,256]{2,1,0:T(8,128)S(1)}, u32[]{:S(2)}, u32[]{:S(2)}) collective-permute-start(f32[2,32,256]{2,1,0:T(8,128)S(1)} %add.91), channel_id=1, source_target_pairs={{2,0},{6,4},{10,8},{14,12},{3,1},{7,5},{11,9},{15,13},{18,16},{22,... | collective-permute-start | bytes 196616 | tf_op jit(solution)/shard_map/ppermute | solution.py:163
  31.3 41.9 %collective-permute-start.8 = (f32[4,64,256]{2,1,0:T(8,128)S(1)}, f32[4,64,256]{2,1,0:T(8,128)S(1)}, u32[]{:S(2)}, u32[]{:S(2)}) collective-permute-start(f32[4,64,256]{2,1,0:T(8,128)S(1)} %slice.149), channel_id=1, source_target_pairs={{14,6},{15,7},{30,22},{31,23},{46,38},{47,39},{62,54},{63,55},{78,... | collective-permute-start | bytes 786440 | tf_op jit(solution)/shard_map/ppermute | solution.py:163
  32.7 41.3 %collective-permute-start.1 = (f32[2,1,256]{2,1,0:T(1,128)S(1)}, f32[2,1,256]{2,1,0:T(1,128)S(1)}, u32[]{:S(2)}, u32[]{:S(2)}) collective-permute-start(f32[2,1,256]{2,1,0:T(1,128)S(1)} %pad_maximum_fusion.3), channel_id=1, source_target_pairs={{0,8},{1,9},{2,10},{3,11},{4,12},{5,13},{6,14},{7,15},{8,0},{9,1},... | collective-permute-start | bytes 6152 | tf_op jit(solution)/shard_map/ppermute | solution.py:163
  71.3 12.8 %collective-permute-start.15 = (f32[256,256]{1,0:T(8,128)S(1)}, f32[256,256]{1,0:T(8,128)S(1)}, u32[]{:S(2)}, u32[]{:S(2)}) collective-permute-start(f32[256,256]{1,0:T(8,128)S(1)} %select_multiply_fusion.2), channel_id=1, source_target_pairs={{192,128},{224,160},{193,129},{225,161},{194,130},{226,162},{195,1... | collective-permute-start | bytes 786440 | tf_op jit(solution)/shard_map/ppermute | solution.py:163
  72.0 12.1 %collective-permute-start.13 = (f32[256,256]{1,0:T(8,128)S(1)}, f32[256,256]{1,0:T(8,128)S(1)}, u32[]{:S(2)}, u32[]{:S(2)}) collective-permute-start(f32[256,256]{1,0:T(8,128)S(1)} %select_multiply_fusion.2), channel_id=1, source_target_pairs={{192,0},{224,32},{193,1},{225,33},{194,2},{226,34},{195,3},{227,35... | collective-permute-start | bytes 786440 | tf_op jit(solution)/shard_map/ppermute | solution.py:163
  73.3 10.8 %collective-permute-start.14 = (f32[256,256]{1,0:T(8,128)S(1)}, f32[256,256]{1,0:T(8,128)S(1)}, u32[]{:S(2)}, u32[]{:S(2)}) collective-permute-start(f32[256,256]{1,0:T(8,128)S(1)} %select_multiply_fusion.2), channel_id=1, source_target_pairs={{192,64},{224,96},{193,65},{225,97},{194,66},{226,98},{195,67},{22... | collective-permute-start | bytes 786440 | tf_op jit(solution)/shard_map/ppermute | solution.py:163
  74.0 8.7 %collective-permute-start.9 = (f32[4,32,256]{2,1,0:T(8,128)S(1)}, f32[4,32,256]{2,1,0:T(8,128)S(1)}, u32[]{:S(2)}, u32[]{:S(2)}) collective-permute-start(f32[4,32,256]{2,1,0:T(8,128)S(1)} %slice.151), channel_id=1, source_target_pairs={{6,2},{14,10},{7,3},{15,11},{22,18},{30,26},{23,19},{31,27},{38,34... | collective-permute-start | bytes 393224 | tf_op jit(solution)/shard_map/ppermute | solution.py:163
  75.6 16.4 %all-to-all-start.1 = ((f32[8,2,32,256]{3,2,1,0:T(8,128)}), f32[8,2,32,256]{3,2,1,0:T(8,128)}, u32[]{:S(2)}, u32[]{:S(2)}) async-start(f32[8,2,32,256]{3,2,1,0:T(8,128)} %broadcast_in_dim.25), calls=%async_computation.1 | async-start | bytes 1048576 | tf_op jit(solution)/shard_map/all_to_all | solution.py:169
  82.8 5.4 %collective-permute-start.10 = (f32[4,16,256]{2,1,0:T(8,128)S(1)}, f32[4,16,256]{2,1,0:T(8,128)S(1)}, u32[]{:S(2)}, u32[]{:S(2)}) collective-permute-start(f32[4,16,256]{2,1,0:T(8,128)S(1)} %slice.153), channel_id=1, source_target_pairs={{2,0},{6,4},{10,8},{14,12},{3,1},{7,5},{11,9},{15,13},{18,16},{22,... | collective-permute-start | bytes 196616 | tf_op jit(solution)/shard_map/ppermute | solution.py:163
  84.2 23.4 %collective-permute-start.18 = (f32[256,256]{1,0:T(8,128)S(1)}, f32[256,256]{1,0:T(8,128)}, u32[]{:S(2)}, u32[]{:S(2)}) collective-permute-start(f32[256,256]{1,0:T(8,128)S(1)} %add_select_fusion), channel_id=1, source_target_pairs={{0,32},{32,0},{64,96},{96,64},{128,160},{160,128},{192,224},{224,1... | collective-permute-start | bytes 786440 | tf_op jit(solution)/shard_map/ppermute | solution.py:163
  92.0 17.4 %collective-permute-start.17 = (f32[8,2,32,256]{3,2,1,0:T(8,128)}, f32[8,2,32,256]{3,2,1,0:T(8,128)}, u32[]{:S(2)}, u32[]{:S(2)}) collective-permute-start(f32[8,2,32,256]{3,2,1,0:T(8,128)} %all-to-all-done.1.near_ref), channel_id=1, source_target_pairs={{0,1},{1,0},{2,3},{3,2},{4,5},{5,4},{6,7},{7,6},{8,9},{9,8},{10,11... | collective-permute-start | bytes 1572872 | tf_op jit(solution)/shard_map/ppermute | solution.py:163
  96.7 31.8 %collective-permute-start.16 = (f32[3,256,256]{2,1,0:T(8,128)S(1)}, f32[3,256,256]{2,1,0:T(8,128)S(1)}, u32[]{:S(2)}, u32[]{:S(2)}) collective-permute-start(f32[3,256,256]{2,1,0:T(8,128)S(1)} %subtract_select_fusion), channel_id=1, source_target_pairs={{0,16},{1,17},{2,18},{3,19},{4,20},{5,21},{6,22},{7,23},{8,24},{9,... | collective-permute-start | bytes 2359304 | tf_op jit(solution)/shard_map/ppermute | solution.py:163
  99.4 29.1 %all-to-all-start.2 = ((f32[8,4,16,256]{3,2,1,0:T(8,128)}), f32[8,4,16,256]{3,2,1,0:T(8,128)S(1)}, u32[]{:S(2)}, u32[]{:S(2)}) async-start(f32[8,4,16,256]{3,2,1,0:T(8,128)} %broadcast_in_dim.28), calls=%async_computation.2 | async-start | bytes 1048576 | tf_op jit(solution)/shard_map/all_to_all | solution.py:169
  128.5 14.5 %collective-permute-start.19 = (f32[8,4,16,256]{3,2,1,0:T(8,128)S(1)}, f32[8,4,16,256]{3,2,1,0:T(8,128)S(1)}, u32[]{:S(2)}, u32[]{:S(2)}) collective-permute-start(f32[8,4,16,256]{3,2,1,0:T(8,128)S(1)} %all-to-all-done.2.own_ref), channel_id=1, source_target_pairs={{0,16},{1,17},{2,18},{3,19},{4,20},{5,21},{6,22},{7,23},{8,24},{9,... | collective-permute-start | bytes 1572872 | tf_op jit(solution)/shard_map/ppermute | solution.py:163
  131.5 14.9 %collective-permute-start.20 = (f32[8,4,16,256]{3,2,1,0:T(8,128)S(1)}, f32[8,4,16,256]{3,2,1,0:T(8,128)S(1)}, u32[]{:S(2)}, u32[]{:S(2)}) collective-permute-start(f32[8,4,16,256]{3,2,1,0:T(8,128)S(1)} %all-to-all-done.2.own_ref), channel_id=1, source_target_pairs={{0,1},{1,0},{2,3},{3,2},{4,5},{5,4},{6,7},{7,6},{8,9},{9,8},{10,11... | collective-permute-start | bytes 1572872 | tf_op jit(solution)/shard_map/ppermute | solution.py:163
  143.0 3.4 %collective-permute-start.21 = (f32[8,4,16,256]{3,2,1,0:T(8,128)S(1)}, f32[8,4,16,256]{3,2,1,0:T(8,128)S(1)}, u32[]{:S(2)}, u32[]{:S(2)}) collective-permute-start(f32[8,4,16,256]{3,2,1,0:T(8,128)S(1)} %collective-permute-done.19.across_ref), channel_id=1, source_target_pairs={{0,1},{1,0},{2,3},{3,2},{4,5},{5,4},{6,7},{7,6},{8,9},{9,8},{10,11... | collective-permute-start | bytes 1572872 | tf_op jit(solution)/shard_map/ppermute | solution.py:163
  (13 other events, 22.9 us)
where the time goes:
time: 153 us; the launch traced here: 152 us
  starting transfers between devices  57 us (37%)
  waiting for transfers between devices  50 us (33%)
  Pallas kernels  24 us (16%)
  other arithmetic  12 us (8%)
  local copies, waits for them, and re-layouts  8.86 us (6%)
    ppermute x22, waiting for transfers between devices, send(): return lax.ppermute(value, axis, pairs)  46.2 us
    ppermute x22, starting transfers between devices, send(): return lax.ppermute(value, axis, pairs)  37.5 us
    pallas_call x3, Pallas kernels, call(): pl.pallas_call(kernel, out_shape=out_shape, in_specs=smem + [pl.BlockSpec...  24 us
    all_to_all x3, starting transfers between devices, exchange(): return lax.all_to_all(parts, axis, 0, 0, axis_index_groups=groups)  19.6 us
    unnamed x27, local copies, waits for them, and re-layouts  4.67 us
    all_to_all x3, waiting for transfers between devices, exchange(): return lax.all_to_all(parts, axis, 0, 0, axis_index_groups=groups)  3.77 us
  transfers between devices with their start and end apart: 25, of which 4 were waited for; matrix products, arithmetic and copies ran while one was open for 9% of the time, Pallas kernels for 13%

commit v1 on v0

--- a/solution.py
+++ b/solution.py
@@ -88,9 +88,11 @@
 
 def first_kernel(odd_ref, near_ref, far_ref, first_ref, left_ref, right_ref, schur_ref, p_ref, e_ref):
     odd = odd_ref[0] == 1
+    tall = p_ref.shape[0] // near_ref.shape[0]
 
     def part(i, j):
-        near, far = near_ref[:, i], far_ref[:, i]
+        at = pl.ds(i * tall, tall)
+        near, far = near_ref[:, at], far_ref[:, at]
         return jnp.where(odd == (j == 1), near, far).reshape(p_ref.shape)
 
     p_ref[...] = part(0, 0)
@@ -110,19 +112,26 @@
 
 
 def last_kernel(place_ref, base_ref, own_ref, across_ref, twin_ref, other_ref, rows_ref, out_ref):
-    odd, half = place_ref[0] == 1, place_ref[1]
-    count, blocks, strip, size = own_ref.shape
-    tall = count * strip
+    odd, lower = place_ref[0] == 1, place_ref[1] == 1
+    blocks, size = base_ref.shape[:2]
+    parts = size // 128
+    strip = size // (2 * own_ref.shape[0])
+    skip = own_ref.shape[1] - blocks * strip
+
+    def joined(one_ref, two_ref, a):
+        one = one_ref[:, skip + a * strip : skip + (a + 1) * strip]
+        two = two_ref[:, a * strip : (a + 1) * strip]
+        both = jnp.stack([jnp.where(lower, two, one), jnp.where(lower, one, two)], axis=1)
+        return both.reshape(size, size)
+
     for a in range(blocks):
-        for side, (same, swapped) in enumerate([(own_ref, twin_ref), (across_ref, other_ref)]):
-            one, two = same[:, a].reshape(tall, size), swapped[:, a].reshape(tall, size)
-            update = kdot(jnp.where(odd, two, one), rows_ref[0])
-            update += kdot(jnp.where(odd, one, two), rows_ref[1])
-            top = (half if side == 0 else 1 - half) * tall
-            value = base_ref[a, pl.ds(pl.multiple_of(top, tall), tall), :] - update
-            for lane in range(size // 128):
-                at = pl.ds((a * size + top) * (size // 128) + lane, tall, stride=size // 128)
-                out_ref[at, :] = value[:, lane * 128 : (lane + 1) * 128]
+        same, swapped = joined(own_ref, across_ref, a), joined(twin_ref, other_ref, a)
+        update = kdot(jnp.where(odd, swapped, same), rows_ref[0])
+        update += kdot(jnp.where(odd, same, swapped), rows_ref[1])
+        value = base_ref[a] - update
+        for lane in range(parts):
+            at = pl.ds(a * size * parts + lane, size, stride=parts)
+            out_ref[at, :] = value[:, lane * 128 : (lane + 1) * 128]
 
 
 def call(kernel, out_shape, scratch, flops, *args):
@@ -178,42 +187,41 @@
     top_one, top_two = col // span_one % 2 == 0, col // span_two % 2 == 0
 
     tail = state[last]
-    strips = exchange(tail.reshape(rows, block // rows, block), "row")[rows - 2 :]
-    crossed = send(strips, [(i, i - half) for i in (cols - 2, cols - 1)])
-    both = jnp.where(place == ring - 1, jnp.where(side == 1, strips, crossed), 0.0)
-
-    left = jnp.where(
-        diagonal,
-        jnp.concatenate([state[:last], (tail - identity)[None]], 0),
-        state,
-    )
-    left = butterfly(left, row_scales)
-    tall = block // 2
-    crossed = send(left[:, :tall], [(i, i - half) for i in (cols - 2, cols - 1)])
-    own_half = jnp.where(side == 1, left[:, tall:], after(crossed, both))
-
-    def hops(step):
-        sources = range(2 * step - 1, ring, 2 * step)
-        return [(group[p], group[p - step]) for group in rings for p in sources]
-
-    steps = [ring >> (i + 1) for i in range(ring.bit_length() - 1)]
-
-    ready = [both]
-    for step in steps:
-        ready.append(ready[-1] + send(ready[-1], hops(step)))
-    strips = ready[-1]
-
-    piece = own_half
-    for i, step in enumerate(steps):
-        wide = piece.shape[1] // 2
-        moved = after(send(piece[:, :wide], hops(step)), ready[i + 1])
-        piece = jnp.where(place % (2 * step) == 2 * step - 1, piece[:, wide:], moved)
+    tall = block // ring
+    strips = state.reshape(blocks, ring, tall, block).transpose(1, 0, 2, 3)
+    strips = exchange(strips, "col", rings)[ring - 1]
+    crossing = [(i + half, i) for i in range(half)]
+    planes = [
+        [r * cols + s * half + i for r in range(rows) for s in range(2)] for i in range(half)
+    ]
+    pivot_strip = spread(strips[last], 2 * rows, ("row", "col"), planes)
+    pivot_strip = jnp.stack([pivot_strip[2 * rows - 3], pivot_strip[2 * rows - 1]])
+
+    eye_strip = lax.dynamic_slice_in_dim(identity, place * tall, tall, 0)
+    eye_strip = jnp.where(row - (rows - 2) == core, eye_strip, 0.0)
+    left = jnp.concatenate([strips[:last], (strips[last] - eye_strip)[None]], 0)
+    left = butterfly(left, lax.dynamic_slice_in_dim(row_scales, place * tall, tall, 2))
+    crossed = send(left[:, : tall // 2], crossing)
+    piece = jnp.where(side == 1, left[:, tall // 2 :], crossed)
+    sent = jnp.concatenate([pivot_strip.reshape(2 * tall, block), piece.reshape(-1, block)], 0)
+    pivot_near = spread(sent, ring, "col", rings)
+    pivot_far = flip(pivot_near, 1)
+    left_across = flip(pivot_near[:, 2 * tall :], span_one)
 
     cleared = jnp.where(pivot_col, jnp.where(diagonal, identity, 0.0), tail) * col_scales[0]
     tail_one = joined(top_one, cleared, flip(cleared, span_one)) * root_half
     tail_one = tail_one * col_scales[1]
-    partner = after(flip(tail_one, span_two), strips)
+    partner = after(flip(tail_one, span_two), pivot_strip, piece)
     tail_moved = joined(top_two, tail_one, partner) * root_half
+
+    def begun(value, earlier, later):
+        value = jnp.where(pivot_col, 0.0, value) * col_scales[0]
+        partner = after(flip(value, span_one), *earlier)
+        value = joined(top_one, value, partner) * root_half * col_scales[1]
+        return value, flip(after(value, *later), span_two)
+
+    lead, lead_far = begun(state[:1], (), ())
+    rest, rest_far = begun(state[1:last], (pivot_strip,), (pivot_near,))
 
     def row_fan(step):
         pairs = [(i, (i + 2 * step) % rows) for i in (rows - 2, rows - 1)]
@@ -225,30 +233,13 @@
     odd_row = row % 2 == 1
     pivot_rows = jnp.stack([jnp.where(odd_row, far, near), jnp.where(odd_row, near, far)])
 
-    pivot_near = spread(strips, rows, "row")
-    pivot_near = after(pivot_near, piece, near)
-    pivot_far = flip(pivot_near, 1)
-    left_own = spread(after(piece, pivot_near), ring, "col", rings)
-
-    second = col_scales[1]
-    second_one = flip(second, span_one)
-    near_pair = jnp.stack([second, second_one])
-    far_pair = flip(near_pair, span_two)
-    head = jnp.where(pivot_col, 0.0, state[:last]) * col_scales[0]
-    head_far = after(flip(head, span_two), pivot_near)
-    head_own = joined(top_two, near_pair[0] * head, far_pair[0] * head_far)
-    head_sent = joined(top_two, near_pair[1] * head, far_pair[1] * head_far)
-    head_partner = flip(head_sent, span_one)
-
     matrix = jax.ShapeDtypeStruct((block, block), jnp.float32)
     buffer = pltpu.VMEM((block, block), jnp.float32)
     work = 2 * block**3
     first, below, over, schur = call(
         first_kernel, [matrix] * 4, [buffer] * 2, 160 * work, smem, pivot_near, pivot_far
     )
-    left_own = after(left_own, first)
-    left_across = flip(left_own, span_one)
-    left_twin = flip(left_own, 1)
+    left_other = flip(after(left_across, first), 1)
     right = call(
         second_kernel,
         jax.ShapeDtypeStruct((2, block, block), jnp.float32),
@@ -260,10 +251,9 @@
         over,
         pivot_rows,
     )
-    left_across, head_partner = after(left_across, right), after(head_partner, right)
-    left_other = flip(left_across, 1)
-    head_moved = joined(top_one, head_own, head_partner) * (root_half * root_half)
-    moved = butterfly(jnp.concatenate([head_moved, tail_moved[None]], 0), row_scales)
+    lead = joined(top_two, lead, after(lead_far, right)) * root_half
+    rest = joined(top_two, rest, after(rest_far, right)) * root_half
+    moved = butterfly(jnp.concatenate([lead, rest, tail_moved[None]], 0), row_scales)
     result = call(
         last_kernel,
         jax.ShapeDtypeStruct((blocks * block * block // 128, 128), jnp.float32),
@@ -271,9 +261,9 @@
         6 * 8 * work,
         smem,
         moved,
-        left_own,
+        pivot_near,
         left_across,
-        left_twin,
+        pivot_far,
         left_other,
         right,
     )

time: 153 us -> 166 us (1.085)
  the two profiles are of different devices: /device:TPU:1 before, /device:TPU:9 now
where the time goes in v1:
time: 166 us; the launch traced here: 165 us
  waiting for transfers between devices  83.6 us (50%)
  starting transfers between devices  36.4 us (22%)
  Pallas kernels  24.7 us (15%)
  other arithmetic  11.6 us (7%)
  local copies, waits for them, and re-layouts  8.45 us (5%)
    ppermute x14, waiting for transfers between devices, send(): return lax.ppermute(value, axis, pairs)  59.6 us
    pallas_call x3, Pallas kernels, call(): pl.pallas_call(kernel, out_shape=out_shape, in_specs=smem + [pl.BlockSpec...  24.7 us
    all_to_all x3, waiting for transfers between devices, exchange(): return lax.all_to_all(parts, axis, 0, 0, axis_index_groups=groups)  24 us
    all_to_all x3, starting transfers between devices, exchange(): return lax.all_to_all(parts, axis, 0, 0, axis_index_groups=groups)  18.7 us
    ppermute x14, starting transfers between devices, send(): return lax.ppermute(value, axis, pairs)  17.7 us
    unnamed x16, local copies, waits for them, and re-layouts  4.26 us
  transfers between devices with their start and end apart: 17, of which 6 were waited for; matrix products, arithmetic and copies ran while one was open for 9% of the time, Pallas kernels for 12%

profile of v1, /device:TPU:9, one launch (start us, length us, event | category | flops | bytes accessed | tf_op | source)
XLA Modules:
  0.0 165.1 jit_solution(11311054315870209081)
XLA Ops:
  0.0 1.3 copy.14
  2.4 8.3 %all-to-all-start = ((f32[8,4,32,256]{3,2,1,0:T(8,128)}), f32[8,4,32,256]{3,2,1,0:T(8,128)S(1)}, u32[]{:S(2)}, u32[]{:S(2)}) async-start(f32[8,4,32,256]{3,2,1,0:T(8,128)} %bitcast.71), calls=%async_computation | async-start | bytes 2097152 | tf_op jit(solution)/shard_map/all_to_all | solution.py:178
  12.3 2.7 %collective-permute-start.4 = (f32[256,256]{1,0:T(8,128)}, f32[256,256]{1,0:T(8,128)S(1)}, u32[]{:S(2)}, u32[]{:S(2)}) collective-permute-start(f32[256,256]{1,0:T(8,128)} %fusion.7), channel_id=1, source_target_pairs={{0,16},{1,17},{2,18},{3,19},{4,20},{5,21},{6,22},{7,23},{8,24},{9,... | collective-permute-start | bytes 786440 | tf_op jit(solution)/shard_map/ppermute | solution.py:172
  15.9 24.0 %all-to-all-done = f32[8,4,32,256]{3,2,1,0:T(8,128)S(1)} async-done(((f32[8,4,32,256]{3,2,1,0:T(8,128)}), f32[8,4,32,256]{3,2,1,0:T(8,128)S(1)}, u32[]{:S(2)}, u32[]{:S(2)}) %all-to-all-start) | async-done | bytes 1048608 | tf_op jit(solution)/shard_map/all_to_all | solution.py:178
  40.7 6.8 %all-to-all-start.1 = ((f32[16,32,256]{2,1,0:T(8,128)}), f32[16,32,256]{2,1,0:T(8,128)S(1)}, u32[]{:S(2)}, u32[]{:S(2)}) async-start(f32[16,32,256]{2,1,0:T(8,128)} %broadcast_in_dim.30), calls=%async_computation.1 | async-start | bytes 1048576 | tf_op jit(solution)/shard_map/all_to_all | solution.py:178
  47.9 1.3 collective-permute-start.2
  49.6 7.8 %collective-permute-done.2 = f32[4,16,256]{2,1,0:T(8,128)S(1)} collective-permute-done((f32[4,16,256]{2,1,0:T(8,128)S(1)}, f32[4,16,256]{2,1,0:T(8,128)S(1)}, u32[]{:S(2)}, u32[]{:S(2)}) %collective-permute-start.2) | collective-permute-done | bytes 65568 | tf_op jit(solution)/shard_map/ppermute | solution.py:172
  58.6 3.6 %all-to-all-start.2 = ((f32[8,128,256]{2,1,0:T(8,128)}), f32[8,128,256]{2,1,0:T(8,128)S(1)}, u32[]{:S(2)}, u32[]{:S(2)}) async-start(f32[8,128,256]{2,1,0:T(8,128)} %broadcast_in_dim.33), calls=%async_computation.2 | async-start | bytes 2097152 | tf_op jit(solution)/shard_map/all_to_all | solution.py:178
  64.0 3.0 %collective-permute-start = (f32[1,256,256]{2,0,1:T(1,128)}, f32[1,256,256]{2,0,1:T(1,128)}, u32[]{:S(2)}, u32[]{:S(2)}) collective-permute-start(f32[1,256,256]{2,0,1:T(1,128)} %fusion.5), channel_id=1, source_target_pairs={{0,16},{1,17},{2,18},{3,19},{4,20},{5,21},{6,22},{7,23},{8,24},{9,... | collective-permute-start | bytes 786440 | tf_op jit(solution)/shard_map/ppermute | solution.py:172
  67.1 5.4 %collective-permute-start.5 = (f32[256,256]{1,0:T(8,128)S(1)}, f32[256,256]{1,0:T(8,128)S(1)}, u32[]{:S(2)}, u32[]{:S(2)}) collective-permute-start(f32[256,256]{1,0:T(8,128)S(1)} %select_multiply_fusion.3), channel_id=1, source_target_pairs={{0,8},{1,9},{2,10},{3,11},{4,12},{5,13},{6,14},{7,15},{8,0},{9,1},... | collective-permute-start | bytes 786440 | tf_op jit(solution)/shard_map/ppermute | solution.py:172
  72.4 30.1 %collective-permute-done.5 = f32[256,256]{1,0:T(8,128)S(1)} collective-permute-done((f32[256,256]{1,0:T(8,128)S(1)}, f32[256,256]{1,0:T(8,128)S(1)}, u32[]{:S(2)}, u32[]{:S(2)}) %collective-permute-start.5) | collective-permute-done | bytes 262176 | tf_op jit(solution)/shard_map/ppermute | solution.py:172
  103.3 1.4 collective-permute-start.6
  104.6 1.3 collective-permute-start.7
  107.2 1.4 fusion.3
  108.7 9.8 %collective-permute-done.7 = f32[256,256]{1,0:T(8,128)} collective-permute-done((f32[256,256]{1,0:T(8,128)S(1)}, f32[256,256]{1,0:T(8,128)}, u32[]{:S(2)}, u32[]{:S(2)}) %collective-permute-start.7) | collective-permute-done | bytes 262176 | tf_op jit(solution)/shard_map/ppermute | solution.py:172
  118.5 1.1 add_select_fusion
  119.9 1.1 select_multiply_fusion.1
  121.1 5.2 %collective-permute-done.9 = f32[256,256]{1,0:T(8,128)S(1)} collective-permute-done((f32[256,256]{1,0:T(8,128)S(1)}, f32[256,256]{1,0:T(8,128)S(1)}, u32[]{:S(2)}, u32[]{:S(2)}) %collective-permute-start.9) | collective-permute-done | bytes 262176 | tf_op jit(solution)/shard_map/ppermute | solution.py:172
  128.0 9.7 %shard_map.37 = (f32[256,256]{1,0:T(8,128)}, f32[256,256]{1,0:T(8,128)}, f32[256,256]{1,0:T(8,128)}, f32[256,256]{1,0:T(8,128)}) custom-call(s32[2]{0:T(128)} %pad_add_fusion.odd_ref.place_ref, f32[8,128,256]{2,1,0:T(8,128)} %copy-done.1, f32[8,128,256]{2,1,0:T(8,128)} %collective-permute-done.3.far_ref.twin_ref), custom_call_target="tpu_custom_call" | custom-call | flops 5368709120 | bytes 1048576 | tf_op jit(solution)/shard_map/pallas_call | solution.py:140
  137.7 9.7 %shard_map.38.rows_ref = f32[2,256,256]{2,1,0:T(8,128)} custom-call(f32[256,256]{1,0:T(8,128)} %get-tuple-element.15.schur_ref, f32[256,256]{1,0:T(8,128)} %get-tuple-element.16.first_ref, f32[256,256]{1,0:T(8,128)} %get-tuple-element.17.left_ref, f32[256,256]{1,0:T(8,128)} %get-tuple-element.18.right_ref, f32[2,256,256]{2,1,0:T(8,128)} %pad_maximum_fusion.1.rows_ref), custom_call_target="tpu_custom_call" | custom-call | flops 5368709120 | bytes 1048576 | tf_op jit(solution)/shard_map/pallas_call | solution.py:140
  147.4 6.6 %collective-permute-done.11 = f32[2,256,256]{2,1,0:T(8,128)S(1)} collective-permute-done((f32[2,256,256]{2,1,0:T(8,128)S(1)}, f32[2,256,256]{2,1,0:T(8,128)S(1)}, u32[]{:S(2)}, u32[]{:S(2)}) %collective-permute-start.11) | collective-permute-done | bytes 524320 | tf_op jit(solution)/shard_map/ppermute | solution.py:172
  154.8 1.4 fusion.2
  157.9 1.1 maximum_multiply_fusion.1
  159.8 5.3 %shard_map.39 = f32[2048,128]{1,0:T(8,128)} custom-call(s32[2]{0:T(128)} %pad_add_fusion.odd_ref.place_ref, f32[4,256,256]{2,1,0:T(8,128)} %bitcast.75, f32[8,128,256]{2,1,0:T(8,128)} %copy-done.1, f32[8,64,256]{2,1,0:T(8,128)} %collective-permute-done.12.across_ref, f32[8,128,256]{2,1,0:T(8,128)} %collective-permute-done.3.far_ref.twin_ref, ...), custom_call_target="tpu_custom_call" | custom-call | flops 1610612736 | bytes 1048576 | tf_op jit(solution)/shard_map/pallas_call | solution.py:140
  (79 shorter events, 15.4 us)
Async XLA Ops:
  2.4 8.3 %copy-start = (f32[4,256,1,256]{3,2,1,0:T(1,128)S(1)}, f32[4,256,1,256]{3,2,1,0:T(1,128)}, u32[]{:S(2)}) copy-start(f32[4,256,1,256]{3,2,1,0:T(1,128)} %param.3) | copy-start | bytes 3145732
  2.4 37.5 %all-to-all-start = ((f32[8,4,32,256]{3,2,1,0:T(8,128)}), f32[8,4,32,256]{3,2,1,0:T(8,128)S(1)}, u32[]{:S(2)}, u32[]{:S(2)}) async-start(f32[8,4,32,256]{3,2,1,0:T(8,128)} %bitcast.71), calls=%async_computation | async-start | bytes 2097152 | tf_op jit(solution)/shard_map/all_to_all | solution.py:178
  10.9 0.7 copy-start.5
  12.3 54.6 %collective-permute-start.4 = (f32[256,256]{1,0:T(8,128)}, f32[256,256]{1,0:T(8,128)S(1)}, u32[]{:S(2)}, u32[]{:S(2)}) collective-permute-start(f32[256,256]{1,0:T(8,128)} %fusion.7), channel_id=1, source_target_pairs={{0,16},{1,17},{2,18},{3,19},{4,20},{5,21},{6,22},{7,23},{8,24},{9,... | collective-permute-start | bytes 786440 | tf_op jit(solution)/shard_map/ppermute | solution.py:172
  15.1 0.7 copy-start.4
  40.7 16.8 %all-to-all-start.1 = ((f32[16,32,256]{2,1,0:T(8,128)}), f32[16,32,256]{2,1,0:T(8,128)S(1)}, u32[]{:S(2)}, u32[]{:S(2)}) async-start(f32[16,32,256]{2,1,0:T(8,128)} %broadcast_in_dim.30), calls=%async_computation.1 | async-start | bytes 1048576 | tf_op jit(solution)/shard_map/all_to_all | solution.py:178
  47.9 9.6 %collective-permute-start.2 = (f32[4,16,256]{2,1,0:T(8,128)S(1)}, f32[4,16,256]{2,1,0:T(8,128)S(1)}, u32[]{:S(2)}, u32[]{:S(2)}) collective-permute-start(f32[4,16,256]{2,1,0:T(8,128)S(1)} %slice.167), channel_id=1, source_target_pairs={{16,0},{17,1},{18,2},{19,3},{20,4},{21,5},{22,6},{23,7},{24,8},{25... | collective-permute-start | bytes 196616 | tf_op jit(solution)/shard_map/ppermute | solution.py:172
  58.6 48.0 %all-to-all-start.2 = ((f32[8,128,256]{2,1,0:T(8,128)}), f32[8,128,256]{2,1,0:T(8,128)S(1)}, u32[]{:S(2)}, u32[]{:S(2)}) async-start(f32[8,128,256]{2,1,0:T(8,128)} %broadcast_in_dim.33), calls=%async_computation.2 | async-start | bytes 2097152 | tf_op jit(solution)/shard_map/all_to_all | solution.py:178
  63.0 45.5 %collective-permute-start.10 = (f32[2,256,256]{2,1,0:T(8,128)}, f32[2,256,256]{2,1,0:T(8,128)}, u32[]{:S(2)}, u32[]{:S(2)}) collective-permute-start(f32[2,256,256]{2,1,0:T(8,128)} %bitcast_multiply_fusion), channel_id=1, source_target_pairs={{0,16},{1,17},{2,18},{3,19},{4,20},{5,21},{6,22},{7,23},{8,24},{9,... | collective-permute-start | bytes 1572872 | tf_op jit(solution)/shard_map/ppermute | solution.py:172
  64.0 42.6 %collective-permute-start = (f32[1,256,256]{2,0,1:T(1,128)}, f32[1,256,256]{2,0,1:T(1,128)}, u32[]{:S(2)}, u32[]{:S(2)}) collective-permute-start(f32[1,256,256]{2,0,1:T(1,128)} %fusion.5), channel_id=1, source_target_pairs={{0,16},{1,17},{2,18},{3,19},{4,20},{5,21},{6,22},{7,23},{8,24},{9,... | collective-permute-start | bytes 786440 | tf_op jit(solution)/shard_map/ppermute | solution.py:172
  67.1 35.5 %collective-permute-start.5 = (f32[256,256]{1,0:T(8,128)S(1)}, f32[256,256]{1,0:T(8,128)S(1)}, u32[]{:S(2)}, u32[]{:S(2)}) collective-permute-start(f32[256,256]{1,0:T(8,128)S(1)} %select_multiply_fusion.3), channel_id=1, source_target_pairs={{0,8},{1,9},{2,10},{3,11},{4,12},{5,13},{6,14},{7,15},{8,0},{9,1},... | collective-permute-start | bytes 786440 | tf_op jit(solution)/shard_map/ppermute | solution.py:172
  102.6 6.1 %collective-permute-start.8 = (f32[256,256]{1,0:T(8,128)S(1)}, f32[256,256]{1,0:T(8,128)S(1)}, u32[]{:S(2)}, u32[]{:S(2)}) collective-permute-start(f32[256,256]{1,0:T(8,128)S(1)} %select_multiply_fusion.2), channel_id=1, source_target_pairs={{192,128},{224,160},{193,129},{225,161},{194,130},{226,162},{195,1... | collective-permute-start | bytes 786440 | tf_op jit(solution)/shard_map/ppermute | solution.py:172
  103.3 5.4 %collective-permute-start.6 = (f32[256,256]{1,0:T(8,128)S(1)}, f32[256,256]{1,0:T(8,128)}, u32[]{:S(2)}, u32[]{:S(2)}) collective-permute-start(f32[256,256]{1,0:T(8,128)S(1)} %select_multiply_fusion.2), channel_id=1, source_target_pairs={{192,0},{224,32},{193,1},{225,33},{194,2},{226,34},{195,3},{227,35... | collective-permute-start | bytes 786440 | tf_op jit(solution)/shard_map/ppermute | solution.py:172
  104.6 13.8 %collective-permute-start.7 = (f32[256,256]{1,0:T(8,128)S(1)}, f32[256,256]{1,0:T(8,128)}, u32[]{:S(2)}, u32[]{:S(2)}) collective-permute-start(f32[256,256]{1,0:T(8,128)S(1)} %select_multiply_fusion.2), channel_id=1, source_target_pairs={{192,64},{224,96},{193,65},{225,97},{194,66},{226,98},{195,67},{22... | collective-permute-start | bytes 786440 | tf_op jit(solution)/shard_map/ppermute | solution.py:172
  106.6 20.6 %copy-start.1 = (f32[8,128,256]{2,1,0:T(8,128)}, f32[8,128,256]{2,1,0:T(8,128)S(1)}, u32[]{:S(2)}) copy-start(f32[8,128,256]{2,1,0:T(8,128)S(1)} %all-to-all-done.2.near_ref.own_ref) | copy-start | bytes 3145732
  106.6 21.4 %collective-permute-start.3 = (f32[8,128,256]{2,1,0:T(8,128)S(1)}, f32[8,128,256]{2,1,0:T(8,128)}, u32[]{:S(2)}, u32[]{:S(2)}) collective-permute-start(f32[8,128,256]{2,1,0:T(8,128)S(1)} %all-to-all-done.2.near_ref.own_ref), channel_id=1, source_target_pairs={{0,1},{1,0},{2,3},{3,2},{4,5},{5,4},{6,7},{7,6},{8,9},{9,8},{10,11... | collective-permute-start | bytes 3145736 | tf_op jit(solution)/shard_map/ppermute | solution.py:172
  108.5 46.3 %collective-permute-start.1 = (f32[1,256,256]{2,0,1:T(1,128)S(1)}, f32[1,256,256]{2,0,1:T(1,128)}, u32[]{:S(2)}, u32[]{:S(2)}) collective-permute-start(f32[1,256,256]{2,0,1:T(1,128)S(1)} %fusion.3), channel_id=1, source_target_pairs={{0,8},{1,9},{2,10},{3,11},{4,12},{5,13},{6,14},{7,15},{8,0},{9,1},... | collective-permute-start | bytes 786440 | tf_op jit(solution)/shard_map/ppermute | solution.py:172
  119.6 6.7 %collective-permute-start.9 = (f32[256,256]{1,0:T(8,128)S(1)}, f32[256,256]{1,0:T(8,128)S(1)}, u32[]{:S(2)}, u32[]{:S(2)}) collective-permute-start(f32[256,256]{1,0:T(8,128)S(1)} %add_select_fusion), channel_id=1, source_target_pairs={{0,32},{32,0},{64,96},{96,64},{128,160},{160,128},{192,224},{224,1... | collective-permute-start | bytes 786440 | tf_op jit(solution)/shard_map/ppermute | solution.py:172
  127.1 26.9 %collective-permute-start.11 = (f32[2,256,256]{2,1,0:T(8,128)S(1)}, f32[2,256,256]{2,1,0:T(8,128)S(1)}, u32[]{:S(2)}, u32[]{:S(2)}) collective-permute-start(f32[2,256,256]{2,1,0:T(8,128)S(1)} %select_multiply_fusion.1), channel_id=1, source_target_pairs={{0,8},{1,9},{2,10},{3,11},{4,12},{5,13},{6,14},{7,15},{8,0},{9,1},... | collective-permute-start | bytes 1572872 | tf_op jit(solution)/shard_map/ppermute | solution.py:172
  128.0 28.3 %collective-permute-start.12 = (f32[8,64,256]{2,1,0:T(8,128)}, f32[8,64,256]{2,1,0:T(8,128)}, u32[]{:S(2)}, u32[]{:S(2)}) collective-permute-start(f32[8,64,256]{2,1,0:T(8,128)} %slice.174), channel_id=1, source_target_pairs={{0,16},{1,17},{2,18},{3,19},{4,20},{5,21},{6,22},{7,23},{8,24},{9,... | collective-permute-start | bytes 1572872 | tf_op jit(solution)/shard_map/ppermute | solution.py:172
  154.0 0.8 copy-start.2
  154.8 1.4 copy-start.3
  156.3 2.7 %collective-permute-start.13 = (f32[8,64,256]{2,1,0:T(8,128)}, f32[8,64,256]{2,1,0:T(8,128)S(1)}, u32[]{:S(2)}, u32[]{:S(2)}) collective-permute-start(f32[8,64,256]{2,1,0:T(8,128)} %collective-permute-done.12.across_ref), channel_id=1, source_target_pairs={{0,1},{1,0},{2,3},{3,2},{4,5},{5,4},{6,7},{7,6},{8,9},{9,8},{10,11... | collective-permute-start | bytes 1572872 | tf_op jit(solution)/shard_map/ppermute | solution.py:172
  159.0 0.8 copy-start.6

commit v2 on v1

--- a/solution.py
+++ b/solution.py
@@ -38,10 +38,10 @@
     size = p_ref.shape[0]
     scale = 1.0 / jnp.max(jnp.abs(p_ref[...]))
     p_ref[...] = p_ref[...] * scale
-    gram = kdot(p_ref[...], p_ref[...], (((1,), (1,)), ((), ())))
-    factor = 1.9 / jnp.max(jnp.sum(jnp.abs(gram), axis=0, keepdims=True))
-
-    def start():
+
+    def start(precision):
+        gram = kdot(p_ref[...], p_ref[...], (((1,), (1,)), ((), ())), precision)
+        factor = 1.9 / jnp.max(jnp.sum(jnp.abs(gram), axis=0, keepdims=True))
         x_ref[...] = p_ref[...].T * factor
 
     def residual(precision):
@@ -58,7 +58,7 @@
         e = e_ref[...]
         return jnp.sum(e * e)
 
-    start()
+    start(lax.Precision.DEFAULT)
 
     @pl.loop(0, WARM)
     def _(_):
@@ -70,7 +70,7 @@
 
     @pl.when(failed)
     def _():
-        start()
+        start(HIGHEST)
         residual(HIGHEST)
 
     def unfinished(carry):
@@ -205,8 +205,10 @@
     piece = jnp.where(side == 1, left[:, tall // 2 :], crossed)
     sent = jnp.concatenate([pivot_strip.reshape(2 * tall, block), piece.reshape(-1, block)], 0)
     pivot_near = spread(sent, ring, "col", rings)
-    pivot_far = flip(pivot_near, 1)
-    left_across = flip(pivot_near[:, 2 * tall :], span_one)
+    pivot_far = flip(pivot_near[:, : 2 * tall], 1)
+    left_own = pivot_near[:, 2 * tall :]
+    left_across = flip(left_own, span_one)
+    left_twin = flip(left_own, 1)
 
     cleared = jnp.where(pivot_col, jnp.where(diagonal, identity, 0.0), tail) * col_scales[0]
     tail_one = joined(top_one, cleared, flip(cleared, span_one)) * root_half
@@ -261,9 +263,9 @@
         6 * 8 * work,
         smem,
         moved,
-        pivot_near,
+        left_own,
         left_across,
-        pivot_far,
+        left_twin,
         left_other,
         right,
     )

time: 166 us -> 168 us (1.012)
  waiting for transfers between devices: 83.6 us -> 70.7 us
  starting transfers between devices: 36.4 us -> 48.1 us
  other arithmetic: 11.6 us -> 15 us
    ppermute x14 -> x15, starting transfers between devices: 17.7 us -> 29.4 us  [send(): return lax.ppermute(value, axis, pairs)]
    ppermute x14 -> x15, waiting for transfers between devices: 59.6 us -> 48.9 us  [send(): return lax.ppermute(value, axis, pairs)]
    all_to_all x3, waiting for transfers between devices: 24 us -> 21.8 us  [exchange(): return lax.all_to_all(parts, axis, 0, 0, axis_index_groups=groups)]
    unnamed x16 -> x18, local copies, waits for them, and re-layouts: 4.26 us -> 4.49 us
  transfers between devices with their start and end apart: 17 -> 18, of which waited for: 6 -> 5; matrix products, arithmetic and copies ran while one was open for 9% -> 11% of each run, Pallas kernels for 12% -> 11%
where the time goes in v2:
time: 168 us; the launch traced here: 167 us
  waiting for transfers between devices  70.7 us (42%)
  starting transfers between devices  48.1 us (29%)
  Pallas kernels  23.9 us (14%)
  other arithmetic  15 us (9%)
  local copies, waits for them, and re-layouts  8.83 us (5%)
    ppermute x15, waiting for transfers between devices, send(): return lax.ppermute(value, axis, pairs)  48.9 us
    ppermute x15, starting transfers between devices, send(): return lax.ppermute(value, axis, pairs)  29.4 us
    pallas_call x3, Pallas kernels, call(): pl.pallas_call(kernel, out_shape=out_shape, in_specs=smem + [pl.BlockSpec...  23.9 us
    all_to_all x3, waiting for transfers between devices, exchange(): return lax.all_to_all(parts, axis, 0, 0, axis_index_groups=groups)  21.8 us
    all_to_all x3, starting transfers between devices, exchange(): return lax.all_to_all(parts, axis, 0, 0, axis_index_groups=groups)  18.7 us
    unnamed x18, local copies, waits for them, and re-layouts  4.49 us
  transfers between devices with their start and end apart: 18, of which 5 were waited for; matrix products, arithmetic and copies ran while one was open for 11% of the time, Pallas kernels for 11%

profile of v2, /device:TPU:9, one launch (start us, length us, event | category | flops | bytes accessed | tf_op | source)
XLA Modules:
  0.0 166.9 jit_solution(9025407466919284937)
XLA Ops:
  0.0 1.3 copy.14
  2.4 8.3 %all-to-all-start = ((f32[8,4,32,256]{3,2,1,0:T(8,128)}), f32[8,4,32,256]{3,2,1,0:T(8,128)S(1)}, u32[]{:S(2)}, u32[]{:S(2)}) async-start(f32[8,4,32,256]{3,2,1,0:T(8,128)} %bitcast.71), calls=%async_computation | async-start | bytes 2097152 | tf_op jit(solution)/shard_map/all_to_all | solution.py:178
  12.3 2.7 %collective-permute-start.4 = (f32[256,256]{1,0:T(8,128)}, f32[256,256]{1,0:T(8,128)}, u32[]{:S(2)}, u32[]{:S(2)}) collective-permute-start(f32[256,256]{1,0:T(8,128)} %fusion.7), channel_id=1, source_target_pairs={{0,16},{1,17},{2,18},{3,19},{4,20},{5,21},{6,22},{7,23},{8,24},{9,... | collective-permute-start | bytes 786440 | tf_op jit(solution)/shard_map/ppermute | solution.py:172
  18.1 21.8 %all-to-all-done = f32[8,4,32,256]{3,2,1,0:T(8,128)S(1)} async-done(((f32[8,4,32,256]{3,2,1,0:T(8,128)}), f32[8,4,32,256]{3,2,1,0:T(8,128)S(1)}, u32[]{:S(2)}, u32[]{:S(2)}) %all-to-all-start) | async-done | bytes 1048608 | tf_op jit(solution)/shard_map/all_to_all | solution.py:178
  40.7 6.8 %all-to-all-start.1 = ((f32[16,32,256]{2,1,0:T(8,128)}), f32[16,32,256]{2,1,0:T(8,128)S(1)}, u32[]{:S(2)}, u32[]{:S(2)}) async-start(f32[16,32,256]{2,1,0:T(8,128)} %broadcast_in_dim.30), calls=%async_computation.1 | async-start | bytes 1048576 | tf_op jit(solution)/shard_map/all_to_all | solution.py:178
  48.6 1.3 collective-permute-start.2
  50.8 3.6 %collective-permute-start = (f32[1,256,256]{2,0,1:T(1,128)}, f32[1,256,256]{2,0,1:T(1,128)}, u32[]{:S(2)}, u32[]{:S(2)}) collective-permute-start(f32[1,256,256]{2,0,1:T(1,128)} %fusion.5), channel_id=1, source_target_pairs={{0,16},{1,17},{2,18},{3,19},{4,20},{5,21},{6,22},{7,23},{8,24},{9,... | collective-permute-start | bytes 786440 | tf_op jit(solution)/shard_map/ppermute | solution.py:172
  54.4 3.1 %collective-permute-done.2 = f32[4,16,256]{2,1,0:T(8,128)S(1)} collective-permute-done((f32[4,16,256]{2,1,0:T(8,128)S(1)}, f32[4,16,256]{2,1,0:T(8,128)S(1)}, u32[]{:S(2)}, u32[]{:S(2)}) %collective-permute-start.2) | collective-permute-done | bytes 65568 | tf_op jit(solution)/shard_map/ppermute | solution.py:172
  58.6 3.6 %all-to-all-start.2 = ((f32[8,128,256]{2,1,0:T(8,128)}), f32[8,128,256]{2,1,0:T(8,128)S(1)}, u32[]{:S(2)}, u32[]{:S(2)}) async-start(f32[8,128,256]{2,1,0:T(8,128)} %broadcast_in_dim.33), calls=%async_computation.2 | async-start | bytes 2097152 | tf_op jit(solution)/shard_map/all_to_all | solution.py:178
  63.3 5.3 %collective-permute-start.5 = (f32[256,256]{1,0:T(8,128)S(1)}, f32[256,256]{1,0:T(8,128)S(1)}, u32[]{:S(2)}, u32[]{:S(2)}) collective-permute-start(f32[256,256]{1,0:T(8,128)S(1)} %select_multiply_fusion.3), channel_id=1, source_target_pairs={{0,8},{1,9},{2,10},{3,11},{4,12},{5,13},{6,14},{7,15},{8,0},{9,1},... | collective-permute-start | bytes 786440 | tf_op jit(solution)/shard_map/ppermute | solution.py:172
  68.7 29.9 %collective-permute-done.5 = f32[256,256]{1,0:T(8,128)S(1)} collective-permute-done((f32[256,256]{1,0:T(8,128)S(1)}, f32[256,256]{1,0:T(8,128)S(1)}, u32[]{:S(2)}, u32[]{:S(2)}) %collective-permute-start.5) | collective-permute-done | bytes 262176 | tf_op jit(solution)/shard_map/ppermute | solution.py:172
  99.3 1.4 collective-permute-start.6
  100.7 1.3 collective-permute-start.7
  102.6 1.4 fusion.3
  104.8 6.4 %collective-permute-done.7 = f32[256,256]{1,0:T(8,128)} collective-permute-done((f32[256,256]{1,0:T(8,128)S(1)}, f32[256,256]{1,0:T(8,128)}, u32[]{:S(2)}, u32[]{:S(2)}) %collective-permute-start.7) | collective-permute-done | bytes 262176 | tf_op jit(solution)/shard_map/ppermute | solution.py:172
  111.2 1.2 add_select_fusion
  113.9 5.4 %collective-permute-start.3 = (f32[8,64,256]{2,1,0:T(8,128)S(1)}, f32[8,64,256]{2,1,0:T(8,128)}, u32[]{:S(2)}, u32[]{:S(2)}) collective-permute-start(f32[8,64,256]{2,1,0:T(8,128)S(1)} %get-tuple-element.30), channel_id=1, source_target_pairs={{0,1},{1,0},{2,3},{3,2},{4,5},{5,4},{6,7},{7,6},{8,9},{9,8},{10,11... | collective-permute-start | bytes 1572872 | tf_op jit(solution)/shard_map/ppermute | solution.py:172
  122.3 3.8 %collective-permute-start.12 = (f32[8,64,256]{2,1,0:T(8,128)}, f32[8,64,256]{2,1,0:T(8,128)S(1)}, u32[]{:S(2)}, u32[]{:S(2)}) collective-permute-start(f32[8,64,256]{2,1,0:T(8,128)} %get-tuple-element.29.own_ref), channel_id=1, source_target_pairs={{0,16},{1,17},{2,18},{3,19},{4,20},{5,21},{6,22},{7,23},{8,24},{9,... | collective-permute-start | bytes 1572872 | tf_op jit(solution)/shard_map/ppermute | solution.py:172
  126.0 2.2 %collective-permute-start.13 = (f32[8,64,256]{2,1,0:T(8,128)}, f32[8,64,256]{2,1,0:T(8,128)S(1)}, u32[]{:S(2)}, u32[]{:S(2)}) collective-permute-start(f32[8,64,256]{2,1,0:T(8,128)} %get-tuple-element.29.own_ref), channel_id=1, source_target_pairs={{0,1},{1,0},{2,3},{3,2},{4,5},{5,4},{6,7},{7,6},{8,9},{9,8},{10,11... | collective-permute-start | bytes 1572872 | tf_op jit(solution)/shard_map/ppermute | solution.py:172
  128.3 9.4 %shard_map.37 = (f32[256,256]{1,0:T(8,128)}, f32[256,256]{1,0:T(8,128)}, f32[256,256]{1,0:T(8,128)}, f32[256,256]{1,0:T(8,128)}) custom-call(s32[2]{0:T(128)} %pad_add_fusion.odd_ref.place_ref, f32[8,128,256]{2,1,0:T(8,128)} %copy-done.1, f32[8,64,256]{2,1,0:T(8,128)} %collective-permute-done.3.far_ref), custom_call_target="tpu_custom_call" | custom-call | flops 5368709120 | bytes 1048576 | tf_op jit(solution)/shard_map/pallas_call | solution.py:140
  137.6 9.5 %shard_map.38.rows_ref = f32[2,256,256]{2,1,0:T(8,128)} custom-call(f32[256,256]{1,0:T(8,128)} %get-tuple-element.15.schur_ref, f32[256,256]{1,0:T(8,128)} %get-tuple-element.16.first_ref, f32[256,256]{1,0:T(8,128)} %get-tuple-element.17.left_ref, f32[256,256]{1,0:T(8,128)} %get-tuple-element.18.right_ref, f32[2,256,256]{2,1,0:T(8,128)} %pad_maximum_fusion.1.rows_ref), custom_call_target="tpu_custom_call" | custom-call | flops 5368709120 | bytes 1048576 | tf_op jit(solution)/shard_map/pallas_call | solution.py:140
  147.1 9.6 %collective-permute-done.11 = f32[2,256,256]{2,1,0:T(8,128)S(1)} collective-permute-done((f32[2,256,256]{2,1,0:T(8,128)S(1)}, f32[2,256,256]{2,1,0:T(8,128)S(1)}, u32[]{:S(2)}, u32[]{:S(2)}) %collective-permute-start.11) | collective-permute-done | bytes 524320 | tf_op jit(solution)/shard_map/ppermute | solution.py:172
  156.7 1.3 fusion.2
  161.9 5.0 %shard_map.39 = f32[2048,128]{1,0:T(8,128)} custom-call(s32[2]{0:T(128)} %pad_add_fusion.odd_ref.place_ref, f32[4,256,256]{2,1,0:T(8,128)} %bitcast.75, f32[8,64,256]{2,1,0:T(8,128)} %get-tuple-element.29.own_ref, f32[8,64,256]{2,1,0:T(8,128)} %copy-done.5, f32[8,64,256]{2,1,0:T(8,128)} %copy-done.6, f32[8,64,256]{2,1,0:T(8,128)} %copy-done.7, ...), custom_call_target="tpu_custom_call" | custom-call | flops 1610612736 | bytes 1048576 | tf_op jit(solution)/shard_map/pallas_call | solution.py:140
  (83 shorter events, 21.1 us)
Async XLA Ops:
  2.4 8.3 %copy-start = (f32[4,256,1,256]{3,2,1,0:T(1,128)S(1)}, f32[4,256,1,256]{3,2,1,0:T(1,128)}, u32[]{:S(2)}) copy-start(f32[4,256,1,256]{3,2,1,0:T(1,128)} %param.3) | copy-start | bytes 3145732
  2.4 37.5 %all-to-all-start = ((f32[8,4,32,256]{3,2,1,0:T(8,128)}), f32[8,4,32,256]{3,2,1,0:T(8,128)S(1)}, u32[]{:S(2)}, u32[]{:S(2)}) async-start(f32[8,4,32,256]{3,2,1,0:T(8,128)} %bitcast.71), calls=%async_computation | async-start | bytes 2097152 | tf_op jit(solution)/shard_map/all_to_all | solution.py:178
  12.3 49.9 %collective-permute-start.4 = (f32[256,256]{1,0:T(8,128)}, f32[256,256]{1,0:T(8,128)}, u32[]{:S(2)}, u32[]{:S(2)}) collective-permute-start(f32[256,256]{1,0:T(8,128)} %fusion.7), channel_id=1, source_target_pairs={{0,16},{1,17},{2,18},{3,19},{4,20},{5,21},{6,22},{7,23},{8,24},{9,... | collective-permute-start | bytes 786440 | tf_op jit(solution)/shard_map/ppermute | solution.py:172
  16.4 87.7 %collective-permute-start.10 = (f32[2,256,256]{2,1,0:T(8,128)}, f32[2,256,256]{2,1,0:T(8,128)}, u32[]{:S(2)}, u32[]{:S(2)}) collective-permute-start(f32[2,256,256]{2,1,0:T(8,128)} %bitcast_multiply_fusion), channel_id=1, source_target_pairs={{0,16},{1,17},{2,18},{3,19},{4,20},{5,21},{6,22},{7,23},{8,24},{9,... | collective-permute-start | bytes 1572872 | tf_op jit(solution)/shard_map/ppermute | solution.py:172
  40.7 16.8 %all-to-all-start.1 = ((f32[16,32,256]{2,1,0:T(8,128)}), f32[16,32,256]{2,1,0:T(8,128)S(1)}, u32[]{:S(2)}, u32[]{:S(2)}) async-start(f32[16,32,256]{2,1,0:T(8,128)} %broadcast_in_dim.30), calls=%async_computation.1 | async-start | bytes 1048576 | tf_op jit(solution)/shard_map/all_to_all | solution.py:178
  48.6 8.9 %collective-permute-start.2 = (f32[4,16,256]{2,1,0:T(8,128)S(1)}, f32[4,16,256]{2,1,0:T(8,128)S(1)}, u32[]{:S(2)}, u32[]{:S(2)}) collective-permute-start(f32[4,16,256]{2,1,0:T(8,128)S(1)} %slice.171), channel_id=1, source_target_pairs={{16,0},{17,1},{18,2},{19,3},{20,4},{21,5},{22,6},{23,7},{24,8},{25... | collective-permute-start | bytes 196616 | tf_op jit(solution)/shard_map/ppermute | solution.py:172
  50.8 51.8 %collective-permute-start = (f32[1,256,256]{2,0,1:T(1,128)}, f32[1,256,256]{2,0,1:T(1,128)}, u32[]{:S(2)}, u32[]{:S(2)}) collective-permute-start(f32[1,256,256]{2,0,1:T(1,128)} %fusion.5), channel_id=1, source_target_pairs={{0,16},{1,17},{2,18},{3,19},{4,20},{5,21},{6,22},{7,23},{8,24},{9,... | collective-permute-start | bytes 786440 | tf_op jit(solution)/shard_map/ppermute | solution.py:172
  58.6 54.1 %all-to-all-start.2 = ((f32[8,128,256]{2,1,0:T(8,128)}), f32[8,128,256]{2,1,0:T(8,128)S(1)}, u32[]{:S(2)}, u32[]{:S(2)}) async-start(f32[8,128,256]{2,1,0:T(8,128)} %broadcast_in_dim.33), calls=%async_computation.2 | async-start | bytes 2097152 | tf_op jit(solution)/shard_map/all_to_all | solution.py:178
  63.3 35.2 %collective-permute-start.5 = (f32[256,256]{1,0:T(8,128)S(1)}, f32[256,256]{1,0:T(8,128)S(1)}, u32[]{:S(2)}, u32[]{:S(2)}) collective-permute-start(f32[256,256]{1,0:T(8,128)S(1)} %select_multiply_fusion.3), channel_id=1, source_target_pairs={{0,8},{1,9},{2,10},{3,11},{4,12},{5,13},{6,14},{7,15},{8,0},{9,1},... | collective-permute-start | bytes 786440 | tf_op jit(solution)/shard_map/ppermute | solution.py:172
  98.6 5.5 %collective-permute-start.8 = (f32[256,256]{1,0:T(8,128)S(1)}, f32[256,256]{1,0:T(8,128)S(1)}, u32[]{:S(2)}, u32[]{:S(2)}) collective-permute-start(f32[256,256]{1,0:T(8,128)S(1)} %select_multiply_fusion.2), channel_id=1, source_target_pairs={{192,128},{224,160},{193,129},{225,161},{194,130},{226,162},{195,1... | collective-permute-start | bytes 786440 | tf_op jit(solution)/shard_map/ppermute | solution.py:172
  99.3 4.8 %collective-permute-start.6 = (f32[256,256]{1,0:T(8,128)S(1)}, f32[256,256]{1,0:T(8,128)}, u32[]{:S(2)}, u32[]{:S(2)}) collective-permute-start(f32[256,256]{1,0:T(8,128)S(1)} %select_multiply_fusion.2), channel_id=1, source_target_pairs={{192,0},{224,32},{193,1},{225,33},{194,2},{226,34},{195,3},{227,35... | collective-permute-start | bytes 786440 | tf_op jit(solution)/shard_map/ppermute | solution.py:172
  100.7 10.5 %collective-permute-start.7 = (f32[256,256]{1,0:T(8,128)S(1)}, f32[256,256]{1,0:T(8,128)}, u32[]{:S(2)}, u32[]{:S(2)}) collective-permute-start(f32[256,256]{1,0:T(8,128)S(1)} %select_multiply_fusion.2), channel_id=1, source_target_pairs={{192,64},{224,96},{193,65},{225,97},{194,66},{226,98},{195,67},{22... | collective-permute-start | bytes 786440 | tf_op jit(solution)/shard_map/ppermute | solution.py:172
  104.0 52.7 %collective-permute-start.1 = (f32[1,256,256]{2,0,1:T(1,128)S(1)}, f32[1,256,256]{2,0,1:T(1,128)}, u32[]{:S(2)}, u32[]{:S(2)}) collective-permute-start(f32[1,256,256]{2,0,1:T(1,128)S(1)} %fusion.3), channel_id=1, source_target_pairs={{0,8},{1,9},{2,10},{3,11},{4,12},{5,13},{6,14},{7,15},{8,0},{9,1},... | collective-permute-start | bytes 786440 | tf_op jit(solution)/shard_map/ppermute | solution.py:172
  104.1 0.7 copy-start.2
  112.4 8.1 %collective-permute-start.9 = (f32[256,256]{1,0:T(8,128)S(1)}, f32[256,256]{1,0:T(8,128)}, u32[]{:S(2)}, u32[]{:S(2)}) collective-permute-start(f32[256,256]{1,0:T(8,128)S(1)} %add_select_fusion), channel_id=1, source_target_pairs={{0,32},{32,0},{64,96},{96,64},{128,160},{160,128},{192,224},{224,1... | collective-permute-start | bytes 786440 | tf_op jit(solution)/shard_map/ppermute | solution.py:172
  112.8 1.1 copy-start.1
  113.9 14.4 %collective-permute-start.3 = (f32[8,64,256]{2,1,0:T(8,128)S(1)}, f32[8,64,256]{2,1,0:T(8,128)}, u32[]{:S(2)}, u32[]{:S(2)}) collective-permute-start(f32[8,64,256]{2,1,0:T(8,128)S(1)} %get-tuple-element.30), channel_id=1, source_target_pairs={{0,1},{1,0},{2,3},{3,2},{4,5},{5,4},{6,7},{7,6},{8,9},{9,8},{10,11... | collective-permute-start | bytes 1572872 | tf_op jit(solution)/shard_map/ppermute | solution.py:172
  122.3 35.8 %collective-permute-start.12 = (f32[8,64,256]{2,1,0:T(8,128)}, f32[8,64,256]{2,1,0:T(8,128)S(1)}, u32[]{:S(2)}, u32[]{:S(2)}) collective-permute-start(f32[8,64,256]{2,1,0:T(8,128)} %get-tuple-element.29.own_ref), channel_id=1, source_target_pairs={{0,16},{1,17},{2,18},{3,19},{4,20},{5,21},{6,22},{7,23},{8,24},{9,... | collective-permute-start | bytes 1572872 | tf_op jit(solution)/shard_map/ppermute | solution.py:172
  126.0 34.8 %collective-permute-start.13 = (f32[8,64,256]{2,1,0:T(8,128)}, f32[8,64,256]{2,1,0:T(8,128)S(1)}, u32[]{:S(2)}, u32[]{:S(2)}) collective-permute-start(f32[8,64,256]{2,1,0:T(8,128)} %get-tuple-element.29.own_ref), channel_id=1, source_target_pairs={{0,1},{1,0},{2,3},{3,2},{4,5},{5,4},{6,7},{7,6},{8,9},{9,8},{10,11... | collective-permute-start | bytes 1572872 | tf_op jit(solution)/shard_map/ppermute | solution.py:172
  128.2 28.4 %collective-permute-start.11 = (f32[2,256,256]{2,1,0:T(8,128)S(1)}, f32[2,256,256]{2,1,0:T(8,128)S(1)}, u32[]{:S(2)}, u32[]{:S(2)}) collective-permute-start(f32[2,256,256]{2,1,0:T(8,128)S(1)} %select_multiply_fusion.1), channel_id=1, source_target_pairs={{0,8},{1,9},{2,10},{3,11},{4,12},{5,13},{6,14},{7,15},{8,0},{9,1},... | collective-permute-start | bytes 1572872 | tf_op jit(solution)/shard_map/ppermute | solution.py:172
  158.1 1.1 copy-start.5
  158.1 2.7 %collective-permute-start.14 = (f32[8,64,256]{2,1,0:T(8,128)S(1)}, f32[8,64,256]{2,1,0:T(8,128)S(1)}, u32[]{:S(2)}, u32[]{:S(2)}) collective-permute-start(f32[8,64,256]{2,1,0:T(8,128)S(1)} %collective-permute-done.12.across_ref), channel_id=1, source_target_pairs={{0,1},{1,0},{2,3},{3,2},{4,5},{5,4},{6,7},{7,6},{8,9},{9,8},{10,11... | collective-permute-start | bytes 1572872 | tf_op jit(solution)/shard_map/ppermute | solution.py:172
  160.9 0.8 copy-start.6
  160.9 1.0 copy-start.7
  (2 other events, 1.4 us)
